TPU v7x, 32 devices: a whole 2x2x4 slice. The times are simulated.
32 devices in a mesh: ep: 16 (over z, y, x), tp: 2 (over core).
Axes of the slice: x: 2, y: 2, z: 4, core: 2. Of those that a mesh axis runs over, the one named last changes fastest.
Arguments:
- tokens: bfloat16 [2048, 3584], P('ep', 'tp'), may hold values from -6 to 6
- routes: int32 [2048, 8], P('ep'), may hold values from 0 to 15, all different within a row; in each aligned block of 128 rows (0 to 127, 128 to 255, ...) at most 72 rows name the same one
- gate_levels: int32 [2048, 8], P('ep'), may hold values from 1 to 255
- w_gate: bfloat16 [16, 3584, 1024], P('ep', 'tp'), may hold values from -0.09375 to 0.09375
- w_up: bfloat16 [16, 3584, 1024], P('ep', 'tp'), may hold values from -0.09375 to 0.09375
- w_down: bfloat16 [16, 1024, 3584], P('ep', None, 'tp'), may hold values from -0.1875 to 0.1875
Outputs:
- mixed: bfloat16 [2048, 3584], P('ep', 'tp')
Inputs may be any that keep to these rules, and one draw needn't show every extreme that they name: `routes`: each row names 8 different experts. Among the 128 tokens of one aligned block no expert is named by more than 72 rows, and in every draw some expert is named by exactly 72 rows of some block.
All inputs are finite; a program needn't handle non-finite values.
Results may differ from a plain program's by a relative error of at most 0.0085.
Values may be sent and summed in bfloat16 or wider, within the bound.
A program may use at most 64 MiB of HBM per device.

v0:
```python
import jax
import jax.numpy as jnp
from jax import lax
from jax.sharding import PartitionSpec as P


def run_expert(inputs, gate_w, up_w, down_w):
    gate_part = jnp.dot(inputs, gate_w, preferred_element_type=jnp.float32)
    up_part = jnp.dot(inputs, up_w, preferred_element_type=jnp.float32)
    gate_sum, up_sum = (
        lax.psum_scatter(gate_part, "tp", scatter_dimension=1, tiled=True),
        lax.psum_scatter(up_part, "tp", scatter_dimension=1, tiled=True),
    )
    hidden = (jax.nn.silu(gate_sum) * up_sum).astype(jnp.bfloat16)
    output = jnp.dot(
        lax.all_gather(hidden, "tp", axis=1, tiled=True), down_w, preferred_element_type=jnp.float32
    )
    return output.astype(jnp.bfloat16)


def on_device(tokens, routes, gate_levels, w_gate, w_up, w_down):
    ep_count = lax.axis_size("ep")
    tok_rows, top_count = routes.shape
    experts_here = w_gate.shape[0]
    capacity = min(tok_rows, max(2, 9 * tok_rows * top_count // (8 * experts_here * ep_count)))
    width_local = tokens.shape[1]
    slots_each = ep_count * capacity
    slots_total = experts_here * slots_each
    flat_ids = routes.reshape(-1)
    positions = jnp.arange(tok_rows * top_count, dtype=jnp.int32)
    same_expert = flat_ids[:, None] == flat_ids[None, :]
    earlier = positions[:, None] > positions[None, :]
    slot_index = jnp.sum(same_expert & earlier, axis=1)
    destination = (
        flat_ids % experts_here * ep_count + flat_ids // experts_here
    ) * capacity + slot_index
    slot_numbers = jnp.arange(slots_total, dtype=jnp.int32)
    matches = destination.reshape(tok_rows, top_count)[:, :, None] == slot_numbers[None, None, :]
    token_slots = jnp.any(matches, axis=1).astype(jnp.bfloat16)
    outgoing = jnp.einsum(
        "ts,td->sd", token_slots, tokens, preferred_element_type=jnp.float32
    ).astype(jnp.bfloat16)
    levels = gate_levels.astype(jnp.float32)
    weights = levels / jnp.sum(levels, axis=1, keepdims=True)
    weight_high = weights.astype(jnp.bfloat16).astype(jnp.float32)
    weight_low = weights - weight_high
    table_high = jnp.sum(jnp.where(matches, weight_high[:, :, None], 0.0), axis=1).astype(
        jnp.bfloat16
    )
    table_low = jnp.sum(jnp.where(matches, weight_low[:, :, None], 0.0), axis=1).astype(
        jnp.bfloat16
    )
    arrived = lax.all_to_all(
        outgoing.reshape(experts_here, ep_count, capacity, width_local),
        "ep",
        split_axis=1,
        concat_axis=1,
        tiled=True,
    )
    expert_rows = arrived.reshape(experts_here, slots_each, width_local)
    results = [run_expert(expert_rows[0], w_gate[0], w_up[0], w_down[0])]
    produced = jnp.stack(results)
    returned = lax.all_to_all(
        produced.reshape(experts_here, ep_count, capacity, width_local),
        "ep",
        split_axis=1,
        concat_axis=1,
        tiled=True,
    )
    flat_returned = returned.reshape(slots_total, width_local)
    mixed = jnp.dot(table_high, flat_returned, preferred_element_type=jnp.float32)
    mixed = mixed + jnp.dot(table_low, flat_returned, preferred_element_type=jnp.float32)
    return mixed.astype(jnp.bfloat16)


def solution(mesh):
    in_specs = (
        P("ep", "tp"),
        P("ep", None),
        P("ep", None),
        P("ep", "tp", None),
        P("ep", "tp", None),
        P("ep", None, "tp"),
    )
    out_specs = P("ep", "tp")
    return jax.shard_map(
        on_device, mesh=mesh, in_specs=in_specs, out_specs=out_specs, check_vma=False
    )
```

profile of v0, /device:TPU:14, one launch (start us, length us, event | category | flops | bytes accessed | tf_op | source)
XLA Modules:
  0.0 286.4 jit_solution(4687454529718250434)
XLA Ops:
  6.5 0.0 copy-start
  6.5 0.0 reduce-scatter.3.cloned.1.call-start
  6.5 0.8 copy.29
  7.4 0.1 eq.30
  7.5 0.5 convert_reduce_fusion
  8.0 0.1 reduce_sum.39
  8.1 0.7 multiply_add_fusion
  8.9 0.1 copy.31
  9.0 1.5 fusion
  10.4 0.0 copy-done
  10.5 1.3 convolution_convert_fusion.1
  11.7 0.0 copy-start.3
  11.8 97.5 %all_to_all.10 = bf16[1,16,72,1792]{3,2,0,1:T(8,128)(2,1)S(1)} all-to-all(bf16[1,16,72,1792]{3,2,0,1:T(8,128)(2,1)S(1)} %bitcast.26), channel_id=1, replica_groups=mesh['ep'=16,'tp'=2] {'ep'}, dimensions={1} | all-to-all | bytes 8257536 | tf_op jit(solution)/shard_map/all_to_all | solution.py:53
  109.2 0.0 copy-start.1
  109.2 2.0 copy-done.1
  111.2 0.0 copy-done.3
  111.3 6.0 %fusion.5 = f32[1152,1024]{1,0:T(8,128)} fusion(bf16[1152,1792]{1,0:T(8,128)(2,1)S(1)} %bitcast.28, bf16[1,1792,1024]{2,1,0:T(8,128)(2,1)S(1)} %copy-done.3), kind=kOutput, calls=%fused_computation.12 | convolution fusion | flops 4227858432 | bytes 12517376 | tf_op jit(solution)/shard_map/dot_general | solution.py:8
  117.2 0.0 reduce-scatter.3.cloned.1.call-update
  117.3 0.0 reduce-scatter.5.cloned.1.call-start
  117.3 10.6 %fusion.3 = f32[1152,1024]{1,0:T(8,128)} fusion(bf16[1152,1792]{1,0:T(8,128)(2,1)} %bitcast.29, bf16[1,1792,1024]{2,1,0:T(8,128)(2,1)} %param.10), kind=kOutput, calls=%fused_computation.10 | convolution fusion | flops 4227858432 | bytes 12517376 | tf_op jit(solution)/shard_map/dot_general | solution.py:9
  127.9 0.0 reduce-scatter.5.cloned.1.call-update
  127.9 0.2 all-gather.2.cloned.1.call-start
  128.1 2.0 reduce-scatter.3.cloned.1.call-done
  130.1 16.0 %reduce-scatter.5.cloned.1.call-done = f32[1152,512]{1,0:T(8,128)} async-done(((f32[1152,1024]{1,0:T(8,128)}), f32[1152,512]{1,0:T(8,128)}) %reduce-scatter.5.cloned.1.call-update) | async-done | bytes 2359312 | tf_op jit(solution)/shard_map/reduce_scatter | solution.py:12
  146.1 4.2 %multiply_convert_fusion = bf16[1152,512]{1,0:T(8,128)(2,1)} fusion(f32[1152,512]{1,0:T(8,128)} %reduce-scatter.5.cloned.1.call-done, f32[1152,512]{1,0:T(8,128)} %reduce-scatter.3.cloned.1.call-done), kind=kLoop, calls=%fused_computation.16 | loop fusion | flops 3538944 | bytes 5898240 | tf_op jit(solution)/shard_map/convert_element_type | solution.py:14
  150.3 0.0 all-gather.2.cloned.1.call-update
  150.3 12.3 %all-gather.2.cloned.1.call-done = bf16[1152,1024]{1,0:T(8,128)(2,1)} async-done(((bf16[1152,512]{1,0:T(8,128)(2,1)}), bf16[1152,1024]{1,0:T(8,128)(2,1)}) %all-gather.2.cloned.1.call-update) | async-done | bytes 2359312 | tf_op jit(solution)/shard_map/all_gather | solution.py:16
  162.6 9.1 %convolution_convert_fusion = bf16[1152,1792]{1,0:T(8,128)(2,1)} fusion(bf16[1152,1024]{1,0:T(8,128)(2,1)} %all-gather.2.cloned.1.call-done, bf16[1,1024,1792]{2,1,0:T(8,128)(2,1)} %param.11), kind=kOutput, calls=%fused_computation | convolution fusion | flops 4229922816 | bytes 10158080 | tf_op jit(solution)/shard_map/dot_general | solution.py:15
  171.8 0.0 copy-start.2
  171.8 7.1 %all-to-all-start.1 = ((bf16[1,16,72,1792]{3,2,0,1:T(8,128)(2,1)}), bf16[1,16,72,1792]{3,2,0,1:T(8,128)(2,1)}, u32[]{:S(2)}, u32[]{:S(2)}) async-start(bf16[1,16,72,1792]{3,2,0,1:T(8,128)(2,1)} %bitcast.27), calls=%async_computation.3 | async-start | bytes 8257536 | tf_op jit(solution)/shard_map/all_to_all | solution.py:63
  178.8 0.0 copy-done.2
  178.9 0.1 copy.32
  179.0 0.1 copy.35
  179.1 3.1 %select_reduce_fusion = (bf16[128,1152]{1,0:T(8,128)(2,1)S(1)}, bf16[128,1152]{1,0:T(8,128)(2,1)S(1)}) fusion(f32[128,8]{1,0:T(8,128)S(1)} %copy.35, s32[128,8]{1,0:T(8,128)S(1)} %copy.31, f32[128,8]{1,0:T(8,128)S(1)} %copy.32), kind=kLoop, calls=%fused_computation.2 | loop fusion | flops 5603328 | bytes 602112 | tf_op jit(solution)/shard_map/reduce_sum | solution.py:50
  182.2 91.0 %all-to-all-done.1 = bf16[1,16,72,1792]{3,2,0,1:T(8,128)(2,1)} async-done(((bf16[1,16,72,1792]{3,2,0,1:T(8,128)(2,1)}), bf16[1,16,72,1792]{3,2,0,1:T(8,128)(2,1)}, u32[]{:S(2)}, u32[]{:S(2)}) %all-to-all-start.1) | async-done | bytes 4128800 | tf_op jit(solution)/shard_map/all_to_all | solution.py:63
  273.2 2.9 %fusion.12 = f32[128,1792]{1,0:T(8,128)S(1)} fusion(bf16[128,1152]{1,0:T(8,128)(2,1)S(1)} %get-tuple-element.6, bf16[1152,1792]{1,0:T(8,128)(2,1)} %bitcast.8), kind=kOutput, calls=%fused_computation.25 | convolution fusion | flops 528482304 | bytes 5341184 | tf_op jit(solution)/shard_map/dot_general | solution.py:71
  276.2 3.7 %fusion.7 = bf16[128,1792]{1,0:T(8,128)(2,1)} fusion(f32[128,1792]{1,0:T(8,128)S(1)} %fusion.12, bf16[1152,1792]{1,0:T(8,128)(2,1)} %bitcast.8, bf16[128,1152]{1,0:T(8,128)(2,1)S(1)} %get-tuple-element.5), kind=kOutput, calls=%fused_computation.15 | convolution fusion | flops 528941056 | bytes 5799936 | tf_op jit(solution)/shard_map/dot_general | solution.py:72
  (3 shorter events, 0.1 us)
Async XLA Ops:
  6.5 3.9 %copy-start = (bf16[128,1792]{1,0:T(8,128)(2,1)S(1)}, bf16[128,1792]{1,0:T(8,128)(2,1)}, u32[]{:S(2)}) copy-start(bf16[128,1792]{1,0:T(8,128)(2,1)} %param.6) | copy-start | bytes 1376260
  6.5 123.6 %reduce-scatter.3.cloned.1.call-start = ((), (), s32[]{:S(2)}) async-start(), calls=%async_computation.4 | async-start | bytes 7077888 | tf_op jit(solution)/shard_map/reduce_scatter | solution.py:11
  11.7 99.5 %copy-start.3 = (bf16[1,1792,1024]{2,1,0:T(8,128)(2,1)S(1)}, bf16[1,1792,1024]{2,1,0:T(8,128)(2,1)}, u32[]{:S(2)}) copy-start(bf16[1,1792,1024]{2,1,0:T(8,128)(2,1)} %param.9) | copy-start | bytes 11010052
  109.2 2.0 copy-start.1
  117.3 28.9 %reduce-scatter.5.cloned.1.call-start = ((), (), s32[]{:S(2)}) async-start(), calls=%async_computation.5 | async-start | bytes 7077888 | tf_op jit(solution)/shard_map/reduce_scatter | solution.py:12
  127.9 34.7 %all-gather.2.cloned.1.call-start = ((), (), s32[]{:S(2)}) async-start(), calls=%async_computation.6 | async-start | bytes 3538944 | tf_op jit(solution)/shard_map/all_gather | solution.py:16
  171.8 7.1 %copy-start.2 = (s32[128,8]{0,1:T(8,128)S(1)}, s32[128,8]{0,1:T(8,128)}, u32[]{:S(2)}) copy-start(s32[128,8]{0,1:T(8,128)} %param.8) | copy-start | bytes 12292
  171.8 101.4 %all-to-all-start.1 = ((bf16[1,16,72,1792]{3,2,0,1:T(8,128)(2,1)}), bf16[1,16,72,1792]{3,2,0,1:T(8,128)(2,1)}, u32[]{:S(2)}, u32[]{:S(2)}) async-start(bf16[1,16,72,1792]{3,2,0,1:T(8,128)(2,1)} %bitcast.27), calls=%async_computation.3 | async-start | bytes 8257536 | tf_op jit(solution)/shard_map/all_to_all | solution.py:63
Sparse Core Ops, SparseCore 0:
  117.4 12.7 reduce-scatter.2
  132.4 13.6 reduce-scatter.4
  150.5 12.1 all-gather.1
where the time goes:
time: 287 us; the launch traced here: 286 us
  waiting for transfers between devices  121 us (42%)
  blocking collectives  97.5 us (34%)
  matrix products  33.6 us (12%)
  between operations  13.2 us (5%)
  other arithmetic  9.99 us (3%)
  starting transfers between devices  7.35 us (3%)
  local copies, waits for them, and re-layouts  3.42 us (1%)
    all_to_all x1, blocking collectives, on_device(): lax.all_to_all(outgoing.reshape(experts_here, ep_count, capacity, width_l...  97.5 us
    all_to_all x1, waiting for transfers between devices, on_device(): lax.all_to_all(produced.reshape(experts_here, ep_count, capacity, width_l...  91 us
    reduce_scatter x1, waiting for transfers between devices, run_expert(): lax.psum_scatter(up_part, 'tp', scatter_dimension=1, tiled=True)  16 us
    all_gather x1, waiting for transfers between devices, run_expert(): lax.all_gather(hidden, 'tp', axis=1, tiled=True)  12.3 us
    dot_general x1, matrix products, run_expert(): up_part = jnp.dot(inputs, up_w, preferred_element_type=jnp.float32)  10.6 us
    dot_general x1, matrix products, run_expert(): jnp.dot(lax.all_gather(hidden, 'tp', axis=1, tiled=True), down_w, preferr...  9.13 us
    all_to_all x1, starting transfers between devices, on_device(): lax.all_to_all(produced.reshape(experts_here, ep_count, capacity, width_l...  7.09 us
    dot_general x1, matrix products, run_expert(): gate_part = jnp.dot(inputs, gate_w, preferred_element_type=jnp.float32)  5.98 us
  transfers between devices with their start and end apart: 4, of which 4 were waited for; matrix products, arithmetic and copies ran while one was open for 5% of the time, Pallas kernels for 0%

commit v1 on v0

--- a/solution.py
+++ b/solution.py
@@ -60,12 +60,20 @@
     expert_rows = arrived.reshape(experts_here, slots_each, width_local)
     results = [run_expert(expert_rows[0], w_gate[0], w_up[0], w_down[0])]
     produced = jnp.stack(results)
-    returned = lax.all_to_all(
-        produced.reshape(experts_here, ep_count, capacity, width_local),
-        "ep",
-        split_axis=1,
-        concat_axis=1,
-        tiled=True,
+    returned = jnp.concatenate(
+        lax.all_to_all(
+            jnp.stack(
+                jnp.split(
+                    produced.reshape(experts_here, ep_count, capacity, width_local),
+                    lax.axis_size("ep"),
+                    axis=1,
+                )
+            ),
+            "ep",
+            0,
+            0,
+        ),
+        axis=1,
     )
     flat_returned = returned.reshape(slots_total, width_local)
     mixed = jnp.dot(table_high, flat_returned, preferred_element_type=jnp.float32)

time: 287 us -> 296 us (1.031)
  local copies, waits for them, and re-layouts: 3.42 us -> 14.9 us
    unnamed x9 -> x24, local copies, waits for them, and re-layouts: 2.89 us -> 13.7 us
where the time goes in v1:
time: 296 us
  waiting for transfers between devices  121 us (41%)
  blocking collectives  97.5 us (33%)
  matrix products  31.7 us (11%)
  local copies, waits for them, and re-layouts  14.9 us (5%)
  between operations  13.2 us (4%)
  other arithmetic  9.99 us (3%)
  starting transfers between devices  7.35 us (2%)
    all_to_all x1, blocking collectives, on_device(): lax.all_to_all(outgoing.reshape(experts_here, ep_count, capacity, width_l...  97.5 us
    all_to_all x1, waiting for transfers between devices, on_device(): lax.all_to_all(jnp.stack(jnp.split(produced.reshape(experts_here, ep_coun...  91 us
    reduce_scatter x1, waiting for transfers between devices, run_expert(): lax.psum_scatter(up_part, 'tp', scatter_dimension=1, tiled=True)  16 us
    unnamed x24, local copies, waits for them, and re-layouts  13.7 us
    all_gather x1, waiting for transfers between devices, run_expert(): lax.all_gather(hidden, 'tp', axis=1, tiled=True)  12.3 us
    dot_general x1, matrix products, run_expert(): up_part = jnp.dot(inputs, up_w, preferred_element_type=jnp.float32)  10.6 us
    dot_general x1, matrix products, run_expert(): jnp.dot(lax.all_gather(hidden, 'tp', axis=1, tiled=True), down_w, preferr...  7.2 us
    all_to_all x1, starting transfers between devices, on_device(): lax.all_to_all(jnp.stack(jnp.split(produced.reshape(experts_here, ep_coun...  7.09 us
  transfers between devices with their start and end apart: 4, of which 4 were waited for; matrix products, arithmetic and copies ran while one was open for 5% of the time, Pallas kernels for 0%

profile of v1, /device:TPU:14, one launch (start us, length us, event | category | flops | bytes accessed | tf_op | source)
XLA Modules:
  0.0 296.0 jit_solution(7388869008389958239)
XLA Ops:
  6.5 0.0 copy-start
  6.5 0.0 reduce-scatter.3.cloned.1.call-start
  6.5 0.8 copy.27
  7.4 0.1 eq.30
  7.5 0.5 convert_reduce_fusion
  8.0 0.1 reduce_sum.39
  8.1 0.7 multiply_add_fusion
  8.9 0.1 copy.29
  9.0 1.5 fusion
  10.5 1.3 convolution_convert_fusion.1
  11.7 0.0 copy-start.3
  11.8 97.5 %all_to_all.10 = bf16[1,16,72,1792]{3,2,0,1:T(8,128)(2,1)S(1)} all-to-all(bf16[1,16,72,1792]{3,2,0,1:T(8,128)(2,1)S(1)} %bitcast.88), channel_id=1, replica_groups=mesh['ep'=16,'tp'=2] {'ep'}, dimensions={1} | all-to-all | bytes 8257536 | tf_op jit(solution)/shard_map/all_to_all | solution.py:53
  109.2 2.0 copy-done.1
  111.3 6.0 %fusion.5 = f32[1152,1024]{1,0:T(8,128)} fusion(bf16[1152,1792]{1,0:T(8,128)(2,1)S(1)} %bitcast.105, bf16[1,1792,1024]{2,1,0:T(8,128)(2,1)S(1)} %copy-done.3), kind=kOutput, calls=%fused_computation.12 | convolution fusion | flops 4227858432 | bytes 12517376 | tf_op jit(solution)/shard_map/dot_general | solution.py:8
  117.2 0.0 reduce-scatter.3.cloned.1.call-update
  117.3 0.0 reduce-scatter.5.cloned.1.call-start
  117.3 10.6 %fusion.3 = f32[1152,1024]{1,0:T(8,128)} fusion(bf16[1152,1792]{1,0:T(8,128)(2,1)} %bitcast.106, bf16[1,1792,1024]{2,1,0:T(8,128)(2,1)} %param.10), kind=kOutput, calls=%fused_computation.10 | convolution fusion | flops 4227858432 | bytes 12517376 | tf_op jit(solution)/shard_map/dot_general | solution.py:9
  127.9 0.0 reduce-scatter.5.cloned.1.call-update
  127.9 0.2 all-gather.2.cloned.1.call-start
  128.1 2.0 reduce-scatter.3.cloned.1.call-done
  130.1 16.0 %reduce-scatter.5.cloned.1.call-done = f32[1152,512]{1,0:T(8,128)} async-done(((f32[1152,1024]{1,0:T(8,128)}), f32[1152,512]{1,0:T(8,128)}) %reduce-scatter.5.cloned.1.call-update) | async-done | bytes 2359312 | tf_op jit(solution)/shard_map/reduce_scatter | solution.py:12
  146.1 4.2 %multiply_convert_fusion = bf16[1152,512]{1,0:T(8,128)(2,1)} fusion(f32[1152,512]{1,0:T(8,128)} %reduce-scatter.5.cloned.1.call-done, f32[1152,512]{1,0:T(8,128)} %reduce-scatter.3.cloned.1.call-done), kind=kLoop, calls=%fused_computation.16 | loop fusion | flops 3538944 | bytes 5898240 | tf_op jit(solution)/shard_map/convert_element_type | solution.py:14
  150.3 0.0 all-gather.2.cloned.1.call-update
  150.3 12.3 %all-gather.2.cloned.1.call-done = bf16[1152,1024]{1,0:T(8,128)(2,1)} async-done(((bf16[1152,512]{1,0:T(8,128)(2,1)}), bf16[1152,1024]{1,0:T(8,128)(2,1)}) %all-gather.2.cloned.1.call-update) | async-done | bytes 2359312 | tf_op jit(solution)/shard_map/all_gather | solution.py:16
  162.6 7.2 %convolution_convert_fusion = bf16[1152,1792]{1,0:T(8,128)(2,1)S(1)} fusion(bf16[1152,1024]{1,0:T(8,128)(2,1)} %all-gather.2.cloned.1.call-done, bf16[1,1024,1792]{2,1,0:T(8,128)(2,1)} %param.11), kind=kOutput, calls=%fused_computation | convolution fusion | flops 4229922816 | bytes 10158080 | tf_op jit(solution)/shard_map/dot_general | solution.py:15
  169.8 0.7 fusion.26
  170.5 0.7 fusion.25
  171.3 0.7 fusion.24
  172.0 0.7 fusion.23
  172.7 0.7 fusion.22
  173.4 0.7 fusion.21
  174.2 0.7 fusion.20
  174.9 0.7 fusion.19
  175.6 0.7 fusion.18
  176.3 0.7 fusion.17
  177.0 0.7 fusion.16
  177.8 0.7 fusion.15
  178.5 0.7 fusion.14
  179.2 0.7 fusion.13
  179.9 0.7 fusion.12
  180.6 0.7 fusion.11
  181.3 7.1 %all-to-all-start.1 = ((bf16[16,1,1,72,1792]{4,3,2,1,0:T(8,128)(2,1)}), bf16[16,1,1,72,1792]{4,3,2,1,0:T(8,128)(2,1)}, u32[]{:S(2)}, u32[]{:S(2)}) async-start(bf16[16,1,1,72,1792]{4,3,2,1,0:T(8,128)(2,1)} %fusion.11), calls=%async_computation.3 | async-start | bytes 8257536 | tf_op jit(solution)/shard_map/all_to_all | solution.py:64
  188.5 0.1 copy.30
  188.6 0.1 copy.32
  188.7 3.1 %select_reduce_fusion = (bf16[128,1152]{1,0:T(8,128)(2,1)S(1)}, bf16[128,1152]{1,0:T(8,128)(2,1)S(1)}) fusion(f32[128,8]{1,0:T(8,128)S(1)} %copy.32, s32[128,8]{1,0:T(8,128)S(1)} %copy.29, f32[128,8]{1,0:T(8,128)S(1)} %copy.30), kind=kLoop, calls=%fused_computation.2 | loop fusion | flops 5603328 | bytes 602112 | tf_op jit(solution)/shard_map/reduce_sum | solution.py:50
  191.8 91.0 %all-to-all-done.1 = bf16[16,1,1,72,1792]{4,3,2,1,0:T(8,128)(2,1)} async-done(((bf16[16,1,1,72,1792]{4,3,2,1,0:T(8,128)(2,1)}), bf16[16,1,1,72,1792]{4,3,2,1,0:T(8,128)(2,1)}, u32[]{:S(2)}, u32[]{:S(2)}) %all-to-all-start.1) | async-done | bytes 4128800 | tf_op jit(solution)/shard_map/all_to_all | solution.py:64
  282.8 2.9 fusion.28
  285.7 3.7 %fusion.7 = bf16[128,1792]{1,0:T(8,128)(2,1)} fusion(f32[128,1792]{1,0:T(8,128)S(1)} %fusion.28, bf16[1152,1792]{1,0:T(8,128)(2,1)} %bitcast.23, bf16[128,1152]{1,0:T(8,128)(2,1)S(1)} %get-tuple-element.5), kind=kOutput, calls=%fused_computation.15 | convolution fusion | flops 528941056 | bytes 5799936 | tf_op jit(solution)/shard_map/dot_general | solution.py:80
  (8 shorter events, 0.1 us)
Async XLA Ops:
  6.5 3.9 %copy-start = (bf16[128,1792]{1,0:T(8,128)(2,1)S(1)}, bf16[128,1792]{1,0:T(8,128)(2,1)}, u32[]{:S(2)}) copy-start(bf16[128,1792]{1,0:T(8,128)(2,1)} %param.6) | copy-start | bytes 1376260
  6.5 123.6 %reduce-scatter.3.cloned.1.call-start = ((), (), s32[]{:S(2)}) async-start(), calls=%async_computation.4 | async-start | bytes 7077888 | tf_op jit(solution)/shard_map/reduce_scatter | solution.py:11
  11.7 99.5 %copy-start.3 = (bf16[1,1792,1024]{2,1,0:T(8,128)(2,1)S(1)}, bf16[1,1792,1024]{2,1,0:T(8,128)(2,1)}, u32[]{:S(2)}) copy-start(bf16[1,1792,1024]{2,1,0:T(8,128)(2,1)} %param.9) | copy-start | bytes 11010052
  109.2 2.0 copy-start.1
  117.3 28.9 %reduce-scatter.5.cloned.1.call-start = ((), (), s32[]{:S(2)}) async-start(), calls=%async_computation.5 | async-start | bytes 7077888 | tf_op jit(solution)/shard_map/reduce_scatter | solution.py:12
  127.9 34.7 %all-gather.2.cloned.1.call-start = ((), (), s32[]{:S(2)}) async-start(), calls=%async_computation.6 | async-start | bytes 3538944 | tf_op jit(solution)/shard_map/all_gather | solution.py:16
  181.3 7.1 %copy-start.2 = (s32[128,8]{0,1:T(8,128)S(1)}, s32[128,8]{0,1:T(8,128)}, u32[]{:S(2)}) copy-start(s32[128,8]{0,1:T(8,128)} %param.8) | copy-start | bytes 12292
  181.3 101.4 %all-to-all-start.1 = ((bf16[16,1,1,72,1792]{4,3,2,1,0:T(8,128)(2,1)}), bf16[16,1,1,72,1792]{4,3,2,1,0:T(8,128)(2,1)}, u32[]{:S(2)}, u32[]{:S(2)}) async-start(bf16[16,1,1,72,1792]{4,3,2,1,0:T(8,128)(2,1)} %fusion.11), calls=%async_computation.3 | async-start | bytes 8257536 | tf_op jit(solution)/shard_map/all_to_all | solution.py:64
Sparse Core Ops, SparseCore 0:
  117.4 12.7 reduce-scatter.2
  132.4 13.6 reduce-scatter.4
  150.5 12.1 all-gather.1
